TPU v7x, 32 devices: a whole 2x2x4 slice. The times are simulated.
32 devices in a mesh: gx: 8 (over z, y), gy: 2 (over core), gz: 2 (over x).
Axes of the slice: x: 2, y: 2, z: 4, core: 2. Of those that a mesh axis runs over, the one named last changes fastest.
Arguments:
- adjoint_in: float32 [19, 64, 16, 256], P(None, 'gx', 'gy', 'gz'), may hold values from -16 to 16
- forward_states: float32 [2, 19, 64, 16, 256], P(None, None, 'gx', 'gy', 'gz'), may hold values from 0.01 to 0.63
- design: float32 [64, 16, 256], P('gx', 'gy', 'gz'), may hold values from 0 to 1
- solid_mask: int32 [64, 16, 256], P('gx', 'gy', 'gz'), may hold values 0 or 1
- boundary_kind: int32 [64, 16, 256], P('gx', 'gy', 'gz'), may hold values from 0 to 2, as said below
Outputs:
- adjoint_out: float32 [19, 64, 16, 256], P(None, 'gx', 'gy', 'gz')
- sensitivity: float32 [64, 16, 256], P('gx', 'gy', 'gz')
- objective: float32 [], replicated
- sens_rms: float32 [], replicated
Inputs may be any that keep to these rules, and one draw needn't show every extreme that they name: `boundary_kind`: 1 marks inlet cells, 2 outlet cells.
All inputs are finite; a program needn't handle non-finite values. No bound on the sum of `solid_mask` on one device may be relied on, other than what follows from the above.
Results may differ from a plain program's by a relative error of at most 0.0003.
Values sent between devices are 32-bit elements; how exact they have to be, the bound alone decides.
A program may use at most 64 MiB of HBM per device.

v0:
```python
import functools

import jax
import jax.numpy as jnp
import numpy as np
from jax import lax
from jax.experimental import pallas as pl
from jax.experimental.pallas import tpu as pltpu
from jax.sharding import PartitionSpec as P

MESH = pl.DeviceIdType.MESH
lattice_table = np.array(
    [
        [0, 0, 0],
        [1, 0, 0],
        [-1, 0, 0],
        [0, 1, 0],
        [0, -1, 0],
        [0, 0, 1],
        [0, 0, -1],
        [1, 1, 0],
        [-1, -1, 0],
        [1, -1, 0],
        [-1, 1, 0],
        [1, 0, 1],
        [-1, 0, -1],
        [1, 0, -1],
        [-1, 0, 1],
        [0, 1, 1],
        [0, -1, -1],
        [0, 1, -1],
        [0, -1, 1],
    ],
    dtype=np.int32,
)
LAT = [tuple(int(v) for v in row) for row in lattice_table]
WEIGHTS = np.array([1.0 / 3] + [1.0 / 18] * 6 + [1.0 / 36] * 12, dtype=np.float64)
opposite_index = [0, 2, 1, 4, 3, 6, 5, 8, 7, 10, 9, 12, 11, 14, 13, 16, 15, 18, 17]
inflow_speed = 0.08
AXES = ("gx", "gy", "gz")
VMEM_LIMIT = 16000 * 1024


def moment_rows():
    c = lattice_table.astype(np.float64)
    cx, cy, cz = c[:, 0], c[:, 1], c[:, 2]
    csq = cx * cx + cy * cy + cz * cz
    return np.stack(
        [
            np.ones(19),
            19 * csq - 30,
            (21 * csq * csq - 53 * csq + 24) / 2,
            cx,
            (5 * csq - 9) * cx,
            cy,
            (5 * csq - 9) * cy,
            cz,
            (5 * csq - 9) * cz,
            3 * cx * cx - csq,
            (3 * csq - 5) * (3 * cx * cx - csq),
            cy * cy - cz * cz,
            (3 * csq - 5) * (cy * cy - cz * cz),
            cx * cy,
            cy * cz,
            cx * cz,
            (cy * cy - cz * cz) * cx,
            (cz * cz - cx * cx) * cy,
            (cx * cx - cy * cy) * cz,
        ]
    )


ROWS = moment_rows()
NORMS = np.sum(ROWS * ROWS, axis=1)
SHEAR = 1.0 / 0.6
RATES = [0, 1.19, 1.4, 0, 1.2, 0, 1.2, 0, 1.2, SHEAR, 1.4, SHEAR, 1.4, SHEAR, SHEAR, SHEAR]
RATES = np.array(RATES + [1.98, 1.98, 1.98], dtype=np.float64)


def weighted_rows():
    c = lattice_table.astype(np.float64)
    pairs = [(0, 0), (1, 1), (2, 2), (0, 1), (1, 2), (0, 2)]
    rows = [WEIGHTS] + [WEIGHTS * c[:, a] for a in range(3)]
    rows += [WEIGHTS * c[:, a] * c[:, b] for a, b in pairs]
    out = np.stack(rows) @ (ROWS / NORMS[:, None]).T
    out[np.abs(out) < 1e-12] = 0.0
    return out


WROWS = weighted_rows()


def group(column, sign):
    return [i for i in range(19) if LAT[i][column] == sign]


SLOT = [{i: k for s in (1, -1) for k, i in enumerate(group(col, s))} for col in range(3)]


def side(sign):
    return 0 if sign == 1 else 1


def combine(coefs, terms):
    total = None
    for coef, term in zip(coefs, terms):
        if coef == 0.0:
            continue
        part = term if coef == 1.0 else float(np.float32(coef)) * term
        total = part if total is None else total + part
    return total


def flux_sums(f):
    s = {i: f[i] + f[i + 1] for i in range(1, 19, 2)}
    d = {i: f[i] - f[i + 1] for i in range(1, 19, 2)}
    return s, d


def moments(p):
    s, d = flux_sums(p)
    sxy, sxz, syz = s[7] + s[9], s[11] + s[13], s[15] + s[17]
    axis_yz = s[3] + s[5]
    axis = s[1] + axis_yz
    exy = sxy + sxz
    edge = exy + syz
    m = [None] * 19
    m[0] = p[0] + axis + edge
    m[1] = 8.0 * edge - 11.0 * axis - 30.0 * p[0]
    m[2] = edge - 4.0 * axis + 12.0 * p[0]
    a = 2.0 * s[1] - axis_yz
    b = exy - 2.0 * syz
    m[9] = a + b
    m[10] = b - 2.0 * a
    a = s[3] - s[5]
    b = sxy - sxz
    m[11] = a + b
    m[12] = b - 2.0 * a
    m[13] = s[7] - s[9]
    m[14] = s[15] - s[17]
    m[15] = s[11] - s[13]
    xa, xb = d[7] + d[9], d[11] + d[13]
    ya, yb = d[7] - d[9], d[15] + d[17]
    za, zb = d[11] - d[13], d[15] - d[17]
    for k, axis_d, u, v in ((3, d[1], xa, xb), (5, d[3], ya, yb), (7, d[5], za, zb)):
        e = u + v
        m[k] = axis_d + e
        m[k + 1] = e - 4.0 * axis_d
    m[16] = xa - xb
    m[17] = yb - ya
    m[18] = za - zb
    return m


def rebuild(z):
    out = [None] * 19
    out[0] = z[0] - 30.0 * z[1] + 12.0 * z[2]
    axis = z[0] - 11.0 * z[1] - 4.0 * z[2]
    edge = z[0] + 8.0 * z[1] + z[2]
    px = z[9] - 2.0 * z[10]
    pw = z[11] - 2.0 * z[12]
    qx = z[9] + z[10]
    qw = z[11] + z[12]
    ayz = axis - px
    eyz = edge - 2.0 * qx
    exx = edge + qx
    exy, exz = exx + qw, exx - qw
    jx, jy, jz = z[3] + z[4], z[5] + z[6], z[7] + z[8]
    x1, x2 = jx + z[16], jx - z[16]
    y1, y2 = jy - z[17], jy + z[17]
    z1, z2 = jz + z[18], jz - z[18]
    even = {
        1: axis + 2.0 * px,
        3: ayz + pw,
        5: ayz - pw,
        7: exy + z[13],
        9: exy - z[13],
        11: exz + z[15],
        13: exz - z[15],
        15: eyz + z[14],
        17: eyz - z[14],
    }
    odd = {
        1: z[3] - 4.0 * z[4],
        3: z[5] - 4.0 * z[6],
        5: z[7] - 4.0 * z[8],
        7: x1 + y1,
        9: x1 - y1,
        11: x2 + z1,
        13: x2 - z1,
        15: y2 + z2,
        17: y2 - z2,
    }
    for i in even:
        out[i] = even[i] + odd[i]
        out[i + 1] = even[i] - odd[i]
    return out


def cell_adjoint(f, p, damping, slope, fluid, solid, inner, inlet, outlet, weight):
    s, d = flux_sums(f)
    rho = f[0]
    for i in s:
        rho = rho + s[i]
    fx = d[1] + (d[7] + d[9]) + (d[11] + d[13])
    fy = d[3] + (d[7] - d[9]) + (d[15] + d[17])
    fz = d[5] + (d[11] - d[13]) + (d[15] - d[17])
    inv = 1.0 / rho
    bx, by, bz = fx * inv, fy * inv, fz * inv
    ux, uy, uz = bx * damping, by * damping, bz * damping
    uu = ux * ux + uy * uy + uz * uz
    m = moments(p)
    n = [None] * 19
    for k in range(16):
        rate = float(np.float32(RATES[k]))
        n[k] = m[k] * jnp.where(inner, rate, 1.0) if np.any(WROWS[:, k]) else None
    s0, sx, sy, sz, xx, yy, zz, xy, yz, xz = [
        combine(WROWS[r, :16], n) for r in range(10)
    ]
    vx = jnp.where(inlet, inflow_speed, ux)
    vy = jnp.where(inlet, 0.0, uy)
    vz = jnp.where(inlet, 0.0, uz)
    gx = xx * vx + xy * vy + xz * vz
    gy = xy * vx + yy * vy + yz * vz
    gz = xz * vx + yz * vy + zz * vz
    vv = vx * vx + vy * vy + vz * vz
    rho_bar = (
        s0 * (1.0 - 1.5 * vv)
        + 3.0 * (sx * vx + sy * vy + sz * vz)
        + 4.5 * (gx * vx + gy * vy + gz * vz)
    )
    rho_bar = jnp.where(outlet, 0.0, rho_bar) + (0.5 * weight) * uu
    scale = jnp.where(inlet, 0.0, jnp.where(outlet, 1.0, rho))
    wr = weight * rho
    ux_bar = scale * (3.0 * sx + 9.0 * gx - 3.0 * s0 * vx) + wr * ux
    uy_bar = scale * (3.0 * sy + 9.0 * gy - 3.0 * s0 * vy) + wr * uy
    uz_bar = scale * (3.0 * sz + 9.0 * gz - 3.0 * s0 * vz) + wr * uz
    d_bar = ux_bar * bx + uy_bar * by + uz_bar * bz
    di = damping * inv
    rho_bar = rho_bar - d_bar * di
    z = [None] * 19
    for k in range(19):
        coef = (1.0 - RATES[k]) / NORMS[k]
        z[k] = jnp.where(inner, float(np.float32(coef)) * m[k], 0.0)
    z[0] = z[0] + rho_bar
    z[3] = z[3] + ux_bar * di
    z[5] = z[5] + uy_bar * di
    z[7] = z[7] + uz_bar * di
    out = rebuild(z)
    out = [jnp.where(solid, p[opposite_index[i]], out[i]) for i in range(19)]
    sens = fluid * (d_bar * slope)
    cost = fluid * (0.5 * wr * uu)
    return out, sens, cost


def sum_groups(sizes):
    nx, ny, nz = sizes
    return [nx * ny * nz] if nx * ny * nz <= 64 else [nx, ny * nz]


def kernel(
    sizes,
    adj_hbm,
    fwd_hbm,
    des_hbm,
    sol_hbm,
    kind_hbm,
    out_ref,
    sens_ref,
    tot_ref,
    adj,
    fwd,
    des,
    sol,
    kin,
    mid,
    xs,
    ys,
    zs,
    xr,
    yr,
    zr,
    er,
    load_sem,
    store_sem,
    send_sem,
    recv_sem,
    *sum_refs,
):
    ex, ey, ez = des.shape
    me = tuple(lax.axis_index(name) for name in AXES)
    nx, ny, nz = sizes

    loads = [
        pltpu.make_async_copy(adj_hbm, adj, load_sem.at[0]),
        pltpu.make_async_copy(fwd_hbm.at[1], fwd.at[1], load_sem.at[1]),
        pltpu.make_async_copy(des_hbm, des, load_sem.at[2]),
        pltpu.make_async_copy(sol_hbm, sol, load_sem.at[3]),
        pltpu.make_async_copy(kind_hbm, kin, load_sem.at[4]),
        pltpu.make_async_copy(fwd_hbm.at[0], fwd.at[0], load_sem.at[5]),
    ]
    for load in loads:
        load.start()

    def reach(offset, sign):
        ok = None
        where = {}
        for a in range(3):
            c = sign * offset[a]
            where[AXES[a]] = me[a] + c if c else me[a]
            if c == 1:
                test = me[a] < sizes[a] - 1
            elif c == -1:
                test = me[a] > 0
            else:
                continue
            ok = test if ok is None else jnp.logical_and(ok, test)
        return ok, where

    live = [
        i
        for i in range(1, 19)
        if all(sizes[a] > 1 or LAT[i][a] == 0 for a in range(3))
    ]

    def all_peer(k):
        rank = lax.rem((me[0] * ny + me[1]) * nz + me[2] + k, nx * ny * nz)
        return {
            "gx": rank // (ny * nz),
            "gy": lax.rem(rank // nz, ny),
            "gz": lax.rem(rank, nz),
        }

    def x_peer(k):
        return {"gx": lax.rem(me[0] + k, nx), "gy": me[1], "gz": me[2]}

    def yz_peer(k):
        rank = lax.rem(me[1] * nz + me[2] + k, ny * nz)
        return {"gx": me[0], "gy": rank // nz, "gz": lax.rem(rank, nz)}

    if len(sum_groups(sizes)) == 1:
        peers = [all_peer]
    else:
        peers = [x_peer, yz_peer]

    barrier = pltpu.get_barrier_semaphore()
    count = jnp.int32(sum(n - 1 for n in sum_groups(sizes)))
    for n, peer in zip(sum_groups(sizes), peers):
        for k in range(1, n):
            pl.semaphore_signal(barrier, inc=1, device_id=peer(k), device_id_type=MESH)
    if len(peers) > 1:
        for i in live:
            ok, where = reach(LAT[i], -1)

            @pl.when(ok)
            def _():
                pl.semaphore_signal(barrier, inc=1, device_id=where, device_id_type=MESH)

            count = count + reach(LAT[i], 1)[0].astype(jnp.int32)

    def landing(i, t):
        if i < 3:
            return xr.at[t, i - 1]
        if i < 5:
            return yr.at[t, i - 3]
        if i < 7:
            return zr.at[t, i - 5]
        return er.at[t, i - 7]

    def leaving(i, t):
        c = LAT[i]
        if i < 3:
            return xs.at[t, i - 1]
        if i < 5:
            return ys.at[t, i - 3]
        if i < 7:
            return zs.at[t, i - 5]
        if c[2] == 0:
            return ys.at[t, side(c[1]), SLOT[1][i]]
        return zs.at[t, side(c[2])]

    for i in range(1, 19):
        if i in live:

            @pl.when(jnp.logical_not(reach(LAT[i], 1)[0]))
            def _():
                for t in (0, 1):
                    ref = landing(i, t)
                    ref[...] = jnp.zeros(ref.shape, jnp.float32)

        else:
            for t in (0, 1):
                ref = landing(i, t)
                ref[...] = jnp.zeros(ref.shape, jnp.float32)

    lane = lax.broadcasted_iota(jnp.int32, (ey, ez), 1)
    row = lax.broadcasted_iota(jnp.int32, (ey, ez), 0)

    def hop(i, t):
        ok, where = reach(LAT[i], -1)
        copy = pltpu.make_async_remote_copy(
            src_ref=leaving(i, t),
            dst_ref=landing(i, t),
            send_sem=send_sem.at[t, i - 1],
            recv_sem=recv_sem.at[t, i - 1],
            device_id=where,
            device_id_type=MESH,
        )
        return ok, copy

    def pack_layer(t, x, tiles, packs):
        packs = list(packs)
        for sign in (1, -1):
            h = side(sign)
            if x == (0 if sign == 1 else ex - 1):
                for k, i in enumerate(group(0, sign)):
                    xs[t, h, k] = tiles(i)
            edge = 0 if sign == 1 else ey - 1
            for k, i in enumerate(group(1, sign)):
                ys[t, h, k, x : x + 1, :] = tiles(i)[edge : edge + 1, :]
            edge = 0 if sign == 1 else ez - 1
            for k, i in enumerate(group(2, sign)):
                at = k * ex + x
                moved = tiles(i)
                if (at - edge) % ez:
                    moved = pltpu.roll(moved, (at - edge) % ez, 1)
                packs[h] = jnp.where(lane == at, moved, packs[h])
        return tuple(packs)

    def send_all(t, packs):
        zs[t, 0] = packs[0]
        zs[t, 1] = packs[1]
        for i in sorted(live, key=lambda i: (LAT[i][0] == 0, -sum(map(abs, LAT[i])))):
            ok, copy = hop(i, t)
            pl.when(ok)(copy.start)

    def receive(t, along_x):
        for i in live:
            if (LAT[i][0] != 0) == along_x:
                ok = reach(LAT[i], 1)[0]
                pl.when(ok)(hop(i, t)[1].wait_recv)

    def shifted_columns(t):
        moved = {}
        for i in range(15, 19):
            cy, cz = LAT[i][1], LAT[i][2]
            pack = zr[t, side(cz)]
            src, last = (0, ey - 1) if cy == 1 else (ey - 1, 0)
            corner = er[t, i - 7, src : src + 1, :]
            pack = pltpu.roll(pack, (-cy) % ey, 0)
            moved[i] = jnp.where(row == last, corner, pack)
        return moved

    def pulled_tile(source, t, i, x, moved):
        cx, cy, cz = LAT[i]
        at = x + cx
        inside = 0 <= at < ex
        tile = source[i, at] if inside else xr[t, side(cx), SLOT[0][i]]
        if cy:
            h = side(cy)
            if inside:
                fill = yr[t, h, SLOT[1][i], at : at + 1, :]
            else:
                src = 0 if cx == 1 else ex - 1
                fill = er[t, i - 7, src : src + 1, :]
            last = ey - 1 if cy == 1 else 0
            tile = jnp.where(row == last, fill, pltpu.roll(tile, (-cy) % ey, 0))
        if cz:
            h = side(cz)
            col = SLOT[2][i] * ex
            if cy:
                pack, col = moved[i], col + x
            elif inside:
                pack, col = zr[t, h], col + at
            else:
                pack, col = er[t, i - 7], col + (0 if cx == 1 else ex - 1)
            last = ez - 1 if cz == 1 else 0
            if (last - col) % ez:
                pack = pltpu.roll(pack, (last - col) % ez, 1)
            tile = jnp.where(lane == last, pack, pltpu.roll(tile, (-cz) % ez, 1))
        return tile

    whole_x = nx * ex
    zero = jnp.zeros((ey, ez), jnp.float32)

    def step(t, source, target, packs):
        cost_sum, square_sum = zero, zero
        receive(t, False)
        moved = shifted_columns(t)
        for x in list(range(1, ex - 1)) + [0, ex - 1]:
            if x == 0:
                receive(t, True)
            g = des[x]
            solid = sol[x] == 1
            fluid = jnp.where(solid, 0.0, 1.0)
            kind = kin[x]
            inlet, outlet = kind == 1, kind == 2
            inner = jnp.logical_not(jnp.logical_or(inlet, outlet))
            below = 1.0 / (0.5 + 0.6 * g)
            damping = (0.1 + g) * below
            slope = 0.44 * (below * below)
            place = (me[0] * ex + x).astype(jnp.float32)
            weight = 1.0 + 2.0 * place / (whole_x - 1)
            f = [fwd[t, i, x] for i in range(19)]
            p = [pulled_tile(source, t, i, x, moved) for i in range(19)]
            out, sens, cost = cell_adjoint(
                f, p, damping, slope, fluid, solid, inner, inlet, outlet, weight
            )
            for i in range(19):
                target[i, x] = out[i]
            cost_sum = cost_sum + cost
            if t == 1:
                sens_ref[x] = sens
                packs = pack_layer(0, x, lambda i: out[i], packs)
            else:
                sens = sens + sens_ref[x]
                sens_ref[x] = sens
                square_sum = square_sum + sens * sens
        return cost_sum, square_sum, packs

    loads[0].wait()
    packs = (zero, zero)
    for x in range(ex):
        packs = pack_layer(1, x, lambda i: adj[i, x], packs)
    pl.semaphore_wait(barrier, count)
    send_all(1, packs)
    for load in loads[1:]:
        load.wait()
    cost_one, _, packs = step(1, adj, mid, (zero, zero))
    send_all(0, packs)
    cost_two, square, _ = step(0, mid, out_ref, None)

    half = ez // 2
    cost = jnp.sum(cost_one + cost_two, axis=0, keepdims=True)
    square = jnp.sum(square, axis=0, keepdims=True)
    cost = cost + pltpu.roll(cost, half, 1)
    square = square + pltpu.roll(square, half, 1)
    first = lax.broadcasted_iota(jnp.int32, (1, ez), 1) < half
    total = jnp.where(first, square, cost)

    sent = []
    for r, (n, peer) in enumerate(zip(sum_groups(sizes), peers)):
        part, got, send, recv = sum_refs[4 * r : 4 * r + 4]
        if n == 1:
            continue
        part[...] = total
        copies = []
        for k in range(1, n):
            copy = pltpu.make_async_remote_copy(
                src_ref=part,
                dst_ref=got.at[pl.ds(k - 1, 1)],
                send_sem=send.at[k - 1],
                recv_sem=recv.at[k - 1],
                device_id=peer(k),
                device_id_type=MESH,
            )
            copy.start()
            copies.append(copy)
        got[pl.ds(n - 1, 1)] = total
        for copy in copies:
            copy.wait_recv()
        total = jnp.sum(got[...], axis=0, keepdims=True)
        sent += copies
    cells = nx * ex * ny * ey * nz * ez
    square = jnp.sum(jnp.where(first, total, 0.0), axis=1, keepdims=True)
    cost = jnp.sum(jnp.where(first, 0.0, total), axis=1, keepdims=True)
    rms = jnp.sqrt(square / cells + 1e-06)
    tot_ref[...] = jnp.where(lane == 0, jnp.broadcast_to(cost / cells, (ey, ez)), jnp.broadcast_to(rms, (ey, ez)))
    for t in (1, 0):
        for i in live:
            ok, copy = hop(i, t)
            pl.when(ok)(copy.wait_send)
    for copy in sent:
        copy.wait_send()


def hand_on(adj_in, sens_in, tot_in, adj_out, sens_out, obj_out, rms_out, sens, obj, rms, sem):
    moves = [(adj_in, adj_out), (sens, sens_out), (obj, obj_out), (rms, rms_out)]
    copies = [pltpu.make_async_copy(a, b, sem.at[k]) for k, (a, b) in enumerate(moves)]
    copies[0].start()
    scale = jnp.broadcast_to(1.0 / tot_in[0:1, 1:2], tot_in.shape)
    for x in range(sens.shape[0]):
        sens[x] = sens_in[x] * scale
    copies[1].start()
    obj[0] = tot_in[0, 0]
    rms[0] = tot_in[0, 1]
    copies[2].start()
    copies[3].start()
    for copy in copies:
        copy.wait()


def body(sizes, adjoint_in, forward_states, design, solid_mask, boundary_kind):
    ex, ey, ez = design.shape
    nx, ny, nz = sizes
    any_spec = pl.BlockSpec(memory_space=pltpu.HBM)
    vmem_spec = pl.BlockSpec(memory_space=pltpu.VMEM)
    f32 = jnp.float32
    operands = (adjoint_in, forward_states, design, solid_mask, boundary_kind)
    operands = [pltpu.with_memory_space_constraint(a, pltpu.HBM) for a in operands]
    sum_scratch = []
    for n in sum_groups(sizes):
        sum_scratch += [
            pltpu.VMEM((1, ez), f32),
            pltpu.VMEM((n, ez), f32),
            pltpu.SemaphoreType.DMA((max(n - 1, 1),)),
            pltpu.SemaphoreType.DMA((max(n - 1, 1),)),
        ]
    adjoint, sens, tot = pl.pallas_call(
        functools.partial(kernel, sizes),
        out_shape=(
            jax.ShapeDtypeStruct(adjoint_in.shape, f32),
            jax.ShapeDtypeStruct(design.shape, f32),
            jax.ShapeDtypeStruct((ey, ez), f32),
        ),
        in_specs=[any_spec] * 5,
        out_specs=(vmem_spec, vmem_spec, vmem_spec),
        scratch_shapes=[
            pltpu.VMEM(adjoint_in.shape, f32),
            pltpu.VMEM(forward_states.shape, f32),
            pltpu.VMEM(design.shape, f32),
            pltpu.VMEM(design.shape, jnp.int32),
            pltpu.VMEM(design.shape, jnp.int32),
            pltpu.VMEM(adjoint_in.shape, f32),
            pltpu.VMEM((2, 2, 5, ey, ez), f32),
            pltpu.VMEM((2, 2, 5, ex, ez), f32),
            pltpu.VMEM((2, 2, ey, ez), f32),
            pltpu.VMEM((2, 2, 5, ey, ez), f32),
            pltpu.VMEM((2, 2, 5, ex, ez), f32),
            pltpu.VMEM((2, 2, ey, ez), f32),
            pltpu.VMEM((2, 12, ey, ez), f32),
            pltpu.SemaphoreType.DMA((6,)),
            pltpu.SemaphoreType.DMA,
            pltpu.SemaphoreType.DMA((2, 18)),
            pltpu.SemaphoreType.DMA((2, 18)),
            *sum_scratch,
        ],
        compiler_params=pltpu.CompilerParams(
            collective_id=0, has_side_effects=True, vmem_limit_bytes=VMEM_LIMIT
        ),
    )(*operands)
    adjoint, sens, objective, rms = pl.pallas_call(
        hand_on,
        out_shape=(
            jax.ShapeDtypeStruct(adjoint_in.shape, f32),
            jax.ShapeDtypeStruct(design.shape, f32),
            jax.ShapeDtypeStruct((1,), f32),
            jax.ShapeDtypeStruct((1,), f32),
        ),
        in_specs=[vmem_spec] * 3,
        out_specs=(any_spec, any_spec, any_spec, any_spec),
        scratch_shapes=[
            pltpu.VMEM(design.shape, f32),
            pltpu.SMEM((1,), f32),
            pltpu.SMEM((1,), f32),
            pltpu.SemaphoreType.DMA((4,)),
        ],
        compiler_params=pltpu.CompilerParams(vmem_limit_bytes=VMEM_LIMIT),
    )(adjoint, sens, tot)
    return adjoint, sens, objective.reshape(()), rms.reshape(())


def solution(mesh):
    placed = (
        P(None, "gx", "gy", "gz"),
        P(None, None, "gx", "gy", "gz"),
        P("gx", "gy", "gz"),
        P("gx", "gy", "gz"),
        P("gx", "gy", "gz"),
    )
    return jax.shard_map(
        functools.partial(body, tuple(int(mesh.shape[name]) for name in AXES)),
        mesh=mesh,
        in_specs=placed,
        out_specs=(P(None, "gx", "gy", "gz"), P("gx", "gy", "gz"), P(), P()),
        check_vma=False,
    )
```

profile of v0, /device:TPU:0, one launch (start us, length us, event | category | flops | bytes accessed | tf_op | source)
XLA Modules:
  0.0 20.7 jit_solution(4493463107048295560)
XLA Ops:
  0.6 19.2 %shard_map.84 = (f32[19,8,8,128]{3,2,1,0:T(8,128)S(1)}, f32[8,8,128]{2,1,0:T(8,128)S(1)}, f32[8,128]{1,0:T(8,128)S(1)}) custom-call(f32[19,8,8,128]{3,2,1,0:T(8,128)} %adj_hbm.1, f32[2,19,8,8,128]{4,3,2,1,0:T(8,128)} %fwd_hbm.1, f32[8,8,128]{2,1,0:T(8,128)} %des_hbm.1, s32[8,8,128]{2,1,0:T(8,128)} %sol_hbm.1, s32[8,8,128]{2,1,0:T(8,128)} %kind_hbm.1), custom_call_target="tpu_custom_call" | custom-call | tf_op jit(solution)/shard_map/pallas_call | solution.py:609
  19.8 0.9 %shard_map.85 = (f32[19,8,8,128]{3,2,1,0:T(8,128)}, f32[8,8,128]{2,1,0:T(8,128)}, f32[1]{0:T(128)}, f32[1]{0:T(128)}) custom-call(f32[19,8,8,128]{3,2,1,0:T(8,128)S(1)} %get-tuple-element.11.adj_in, f32[8,8,128]{2,1,0:T(8,128)S(1)} %get-tuple-element.12.sens_in, f32[8,128]{1,0:T(8,128)S(1)} %get-tuple-element.13.tot_in), custom_call_target="tpu_custom_call" | custom-call | tf_op jit(solution)/shard_map/pallas_call | solution.py:642
where the time goes:
time: 20.9 us; the launch traced here: 20.7 us
  Pallas kernels  20.1 us (96%)
  between operations  0.64 us (3%)
    pallas_call x1, Pallas kernels, body(): pl.pallas_call(functools.partial(kernel, sizes), out_shape=(jax.ShapeDtyp...  19.2 us
    pallas_call x1, Pallas kernels, body(): pl.pallas_call(hand_on, out_shape=(jax.ShapeDtypeStruct(adjoint_in.shape,...  0.88 us

commit v1 on v0

--- a/solution.py
+++ b/solution.py
@@ -258,7 +258,7 @@
     return [nx * ny * nz] if nx * ny * nz <= 64 else [nx, ny * nz]
 
 
-def kernel(
+def general_kernel(
     sizes,
     adj_hbm,
     fwd_hbm,
@@ -574,6 +574,338 @@
         copy.wait_send()
 
 
+def near(sizes, cells):
+    nx, ny, nz = sizes
+    return ny == 2 and nz == 2 and nx * ny * nz <= 64 and cells[0] == cells[1]
+
+
+def rounds(nx):
+    return max((nx - 1) // 2, 0)
+
+
+def fast_kernel(
+    sizes,
+    adj_hbm,
+    fwd_hbm,
+    des_hbm,
+    sol_hbm,
+    kind_hbm,
+    out_ref,
+    sens_ref,
+    tot_ref,
+    adj,
+    fwd,
+    des,
+    marks,
+    mid,
+    xs,
+    ys,
+    zs,
+    xr,
+    yr,
+    zr,
+    er,
+    part,
+    got,
+    load_sem,
+    send_sem,
+    side_sem,
+    face_sem,
+    sum_sem,
+    round_sem,
+):
+    ex, ey, ez = des.shape
+    nx, ny, nz = sizes
+    mx, my, mz = (lax.axis_index(name) for name in AXES)
+    oy, oz = 1 - my, 1 - mz
+    has = {1: mx < nx - 1, -1: mx > 0}
+    far = {2: mx < nx - 2, -2: mx > 1}
+
+    loads = [
+        pltpu.make_async_copy(adj_hbm, adj, load_sem.at[0]),
+        pltpu.make_async_copy(fwd_hbm, fwd, load_sem.at[1]),
+        pltpu.make_async_copy(des_hbm, des, load_sem.at[2]),
+        pltpu.make_async_copy(sol_hbm, marks.at[0], load_sem.at[3]),
+        pltpu.make_async_copy(kind_hbm, marks.at[1], load_sem.at[3]),
+    ]
+    loads[0].start()
+
+    barrier = pltpu.get_barrier_semaphore()
+
+    def greet(x, y, z):
+        pl.semaphore_signal(
+            barrier, inc=1, device_id={"gx": x, "gy": y, "gz": z}, device_id_type=MESH
+        )
+
+    for s in (1, -1):
+
+        @pl.when(has[s])
+        def _():
+            for y, z in ((my, oz), (oy, oz), (oy, mz), (my, mz)):
+                greet(mx + s, y, z)
+
+    for y, z in ((my, oz), (oy, oz), (oy, mz)):
+        greet(mx, y, z)
+    for s in (2, -2):
+
+        @pl.when(far[s])
+        def _():
+            greet(mx + s, my, mz)
+
+    far_count = far[2].astype(jnp.int32) + far[-2].astype(jnp.int32)
+    count = 3 + 4 * (has[1].astype(jnp.int32) + has[-1].astype(jnp.int32)) + far_count
+    for load in loads[1:]:
+        load.start()
+
+    def tell(j):
+        for s in (2, -2):
+
+            @pl.when(far[s])
+            def _():
+                pl.semaphore_signal(
+                    round_sem.at[j],
+                    inc=1,
+                    device_id={"gx": mx + s, "gy": my, "gz": mz},
+                    device_id_type=MESH,
+                )
+
+    def hear(j):
+        pl.semaphore_wait(round_sem.at[j], far_count)
+
+    def relay(j):
+        if j < rounds(nx):
+            if j > 0:
+                hear(j - 1)
+            tell(j)
+
+    def clear(ref):
+        ref[...] = jnp.zeros(ref.shape, jnp.float32)
+
+    for t in (0, 1):
+        clear(yr.at[t, oy])
+        clear(zr.at[t, oz])
+        clear(er.at[t, oy, mz])
+        clear(er.at[t, my, oz])
+        clear(er.at[t, oy, oz])
+    for s in (1, -1):
+
+        @pl.when(jnp.logical_not(has[s]))
+        def _():
+            clear(xr.at[side(s)])
+
+    lane = lax.broadcasted_iota(jnp.int32, (ey, ez), 1)
+    row = lax.broadcasted_iota(jnp.int32, (ey, ez), 0)
+    low_z = jnp.broadcast_to(mz == 1, (ey, ez))
+    slot_lane = jnp.where(low_z, lane, jnp.where(lane == ez - 1, 0, lane + 1))
+    match_y = [jnp.broadcast_to(my == h, (1, ez)) for h in (0, 1)]
+    match_z = [jnp.broadcast_to(mz == h, (ey, ez)) for h in (0, 1)]
+
+    def push(src, dst, sent, came, x, y, z):
+        return pltpu.make_async_remote_copy(
+            src_ref=src,
+            dst_ref=dst,
+            send_sem=sent,
+            recv_sem=came,
+            device_id={"gx": x, "gy": y, "gz": z},
+            device_id_type=MESH,
+        )
+
+    def x_sends(t, s):
+        h = side(s)
+        sent, came = send_sem.at[h], face_sem.at[h, t]
+        slot = 1 + oy if s == 1 else 2 - oy
+        return [
+            push(zs.at[t], xr.at[h, t, 6], sent, came, mx - s, my, oz),
+            push(xs.at[t, h], xr.at[h, t, pl.ds(0, 5)], sent, came, mx - s, my, mz),
+            push(ys.at[t, oy, slot], xr.at[h, t, 5], sent, came, mx - s, oy, mz),
+        ]
+
+    def side_sends(t):
+        sent = send_sem.at[2]
+        return [
+            push(zs.at[t], er.at[t, oy, oz], sent, side_sem.at[2, t], mx, oy, oz),
+            push(zs.at[t], zr.at[t, oz], sent, side_sem.at[1, t], mx, my, oz),
+            push(ys.at[t, oy], yr.at[t, oy], sent, side_sem.at[0, t], mx, oy, mz),
+        ]
+
+    def pack_layer(t, x, tiles, pack):
+        for sign in (1, -1):
+            h = side(sign)
+            if x == (0 if sign == 1 else ex - 1):
+                for k, i in enumerate(group(0, sign)):
+                    xs[t, h, k] = tiles(i)
+            edge = 0 if sign == 1 else ey - 1
+            for k, i in enumerate(group(1, sign)):
+                ys[t, h, k, x : x + 1, :] = tiles(i)[edge : edge + 1, :]
+        for k, (i, j) in enumerate(zip(group(2, 1), group(2, -1))):
+            at = k * ex + x
+            moved = jnp.where(low_z, tiles(i), tiles(j))
+            if at % ez:
+                moved = pltpu.roll(moved, at % ez, 1)
+            pack = jnp.where(slot_lane == at, moved, pack)
+        return pack
+
+    def send_all(t, pack):
+        zs[t] = pack
+        for s in (1, -1):
+
+            @pl.when(has[-s])
+            def _():
+                for copy in x_sends(t, s):
+                    copy.start()
+
+        for copy in side_sends(t):
+            copy.start()
+
+    def receive_sides(t):
+        for copy in side_sends(t)[::-1]:
+            copy.wait_recv()
+
+    def receive_face(t, s):
+        h = side(s)
+        ref = xr.at[h, t]
+        copy = push(ref, ref, send_sem.at[h], face_sem.at[h, t], mx, my, mz)
+        pl.when(has[s])(copy.wait_recv)
+
+    def shifted_columns(t):
+        moved = {}
+        for i in range(15, 19):
+            cy, cz = LAT[i][1], LAT[i][2]
+            pack = zr[t, side(cz)]
+            src, last = (0, ey - 1) if cy == 1 else (ey - 1, 0)
+            corner = er[t, side(cy), side(cz), src : src + 1, :]
+            pack = pltpu.roll(pack, (-cy) % ey, 0)
+            moved[i] = jnp.where(row == last, corner, pack)
+        return moved
+
+    def pulled_tile(source, t, i, x, moved):
+        cx, cy, cz = LAT[i]
+        at = x + cx
+        inside = 0 <= at < ex
+        tile = source[i, at] if inside else xr[side(cx), t, SLOT[0][i]]
+        src = 0 if cx == 1 else ex - 1
+        if cy:
+            h = side(cy)
+            if inside:
+                fill = yr[t, h, SLOT[1][i], at : at + 1, :]
+            else:
+                fill = jnp.where(match_y[h], xr[side(cx), t, 5, src : src + 1, :], 0.0)
+            last = ey - 1 if cy == 1 else 0
+            tile = jnp.where(row == last, fill, pltpu.roll(tile, (-cy) % ey, 0))
+        if cz:
+            h = side(cz)
+            col = SLOT[2][i] * ex - h
+            if cy:
+                pack, col = moved[i], col + x
+            elif inside:
+                pack, col = zr[t, h], col + at
+            else:
+                pack = jnp.where(match_z[h], xr[side(cx), t, 6], 0.0)
+                col = col + src
+            last = ez - 1 if cz == 1 else 0
+            if (last - col) % ez:
+                pack = pltpu.roll(pack, (last - col) % ez, 1)
+            tile = jnp.where(lane == last, pack, pltpu.roll(tile, (-cz) % ez, 1))
+        return tile
+
+    whole_x = nx * ex
+    zero = jnp.zeros((ey, ez), jnp.float32)
+
+    def step(t, source, target, pack):
+        cost_sum, square_sum = zero, zero
+        with jax.named_scope(f"sides {t}"):
+            receive_sides(t)
+        if t == 1:
+            relay(1)
+        moved = shifted_columns(t)
+        for x in sorted(range(ex), key=lambda x: x in (0, ex - 1)):
+            with jax.named_scope(f"faces {t}"):
+                if x == 0:
+                    receive_face(t, -1)
+                if x == ex - 1:
+                    receive_face(t, 1)
+            g = des[x]
+            solid = marks[0, x] == 1
+            fluid = jnp.where(solid, 0.0, 1.0)
+            kind = marks[1, x]
+            inlet, outlet = kind == 1, kind == 2
+            inner = jnp.logical_not(jnp.logical_or(inlet, outlet))
+            below = 1.0 / (0.5 + 0.6 * g)
+            damping = (0.1 + g) * below
+            slope = 0.44 * (below * below)
+            place = (mx * ex + x).astype(jnp.float32)
+            weight = 1.0 + 2.0 * place / (whole_x - 1)
+            f = [fwd[t, i, x] for i in range(19)]
+            p = [pulled_tile(source, t, i, x, moved) for i in range(19)]
+            out, sens, cost = cell_adjoint(
+                f, p, damping, slope, fluid, solid, inner, inlet, outlet, weight
+            )
+            for i in range(19):
+                target[i, x] = out[i]
+            cost_sum = cost_sum + cost
+            if t == 1:
+                sens_ref[x] = sens
+                pack = pack_layer(0, x, lambda i: out[i], pack)
+            else:
+                sens = sens + sens_ref[x]
+                sens_ref[x] = sens
+                square_sum = square_sum + sens * sens
+        return cost_sum, square_sum, pack
+
+    with jax.named_scope("load"):
+        loads[0].wait()
+    pack = zero
+    for x in range(ex):
+        pack = pack_layer(1, x, lambda i: adj[i, x], pack)
+    with jax.named_scope("greeted"):
+        pl.semaphore_wait(barrier, count)
+    with jax.named_scope("send 1"):
+        send_all(1, pack)
+        relay(0)
+    for load in loads[1:3]:
+        load.wait()
+    pltpu.make_async_copy(marks, marks, load_sem.at[3]).wait()
+    cost_one, _, pack = step(1, adj, mid, zero)
+    with jax.named_scope("send 0"):
+        send_all(0, pack)
+    for j in range(2, rounds(nx)):
+        relay(j)
+    cost_two, square, _ = step(0, mid, out_ref, None)
+    part[0:1, :] = jnp.sum(square, axis=0, keepdims=True)
+    part[1:2, :] = jnp.sum(cost_one + cost_two, axis=0, keepdims=True)
+
+    with jax.named_scope("heard"):
+        if rounds(nx):
+            hear(rounds(nx) - 1)
+    n = nx * ny * nz
+    with jax.named_scope("send sums"):
+        for dx in sorted(range(nx), key=lambda d: (d == 0, min(d, nx - d))):
+            px = jnp.where(mx + dx >= nx, mx + dx - nx, mx + dx)
+            for dy, dz in ((1, 1), (0, 1), (1, 0), (0, 0)):
+                k = (dx * ny + dy) * nz + dz
+                if k == 0:
+                    continue
+                y, z = (oy if dy else my), (oz if dz else mz)
+                push(part, got.at[k - 1], sum_sem.at[0], sum_sem.at[1], px, y, z).start()
+    got[n - 1] = part[...]
+    every = got.at[pl.ds(0, n - 1)]
+    sums = push(every, every, sum_sem.at[0], sum_sem.at[1], mx, my, mz)
+    with jax.named_scope("sums"):
+        sums.wait_recv()
+    total = jnp.sum(jnp.sum(got[...], axis=0), axis=1, keepdims=True)
+    cells = nx * ex * ny * ey * nz * ez
+    rms = jnp.broadcast_to(jnp.sqrt(total[0:1] / cells + 1e-06), (ey, ez))
+    cost = jnp.broadcast_to(total[1:2] / cells, (ey, ez))
+    tot_ref[...] = jnp.where(lane == 0, cost, rms)
+    with jax.named_scope("drain"):
+        for s in (1, -1):
+            h = side(s)
+            copy = push(xr.at[h], xr.at[h], send_sem.at[h], sum_sem.at[1], mx, my, mz)
+            pl.when(has[-s])(copy.wait_send)
+        push(xr.at[0], xr.at[0], send_sem.at[2], sum_sem.at[1], mx, my, mz).wait_send()
+        sums.wait_send()
+
+
 def hand_on(adj_in, sens_in, tot_in, adj_out, sens_out, obj_out, rms_out, sens, obj, rms, sem):
     moves = [(adj_in, adj_out), (sens, sens_out), (obj, obj_out), (rms, rms_out)]
     copies = [pltpu.make_async_copy(a, b, sem.at[k]) for k, (a, b) in enumerate(moves)]
@@ -598,24 +930,42 @@
     f32 = jnp.float32
     operands = (adjoint_in, forward_states, design, solid_mask, boundary_kind)
     operands = [pltpu.with_memory_space_constraint(a, pltpu.HBM) for a in operands]
-    sum_scratch = []
-    for n in sum_groups(sizes):
-        sum_scratch += [
-            pltpu.VMEM((1, ez), f32),
-            pltpu.VMEM((n, ez), f32),
-            pltpu.SemaphoreType.DMA((max(n - 1, 1),)),
-            pltpu.SemaphoreType.DMA((max(n - 1, 1),)),
+    if near(sizes, design.shape):
+        n = nx * ny * nz
+        run = fast_kernel
+        scratch = [
+            pltpu.VMEM(adjoint_in.shape, f32),
+            pltpu.VMEM(forward_states.shape, f32),
+            pltpu.VMEM(design.shape, f32),
+            pltpu.VMEM((2, *design.shape), jnp.int32),
+            pltpu.VMEM(adjoint_in.shape, f32),
+            pltpu.VMEM((2, 2, 5, ey, ez), f32),
+            pltpu.VMEM((2, 2, 5, ex, ez), f32),
+            pltpu.VMEM((2, ey, ez), f32),
+            pltpu.VMEM((2, 2, 7, ey, ez), f32),
+            pltpu.VMEM((2, 2, 5, ex, ez), f32),
+            pltpu.VMEM((2, 2, ey, ez), f32),
+            pltpu.VMEM((2, 2, 2, ey, ez), f32),
+            pltpu.VMEM((2, ez), f32),
+            pltpu.VMEM((n, 2, ez), f32),
+            pltpu.SemaphoreType.DMA((4,)),
+            pltpu.SemaphoreType.DMA((3,)),
+            pltpu.SemaphoreType.DMA((3, 2)),
+            pltpu.SemaphoreType.DMA((2, 2)),
+            pltpu.SemaphoreType.DMA((2,)),
+            pltpu.SemaphoreType.REGULAR((max(rounds(nx), 1),)),
         ]
-    adjoint, sens, tot = pl.pallas_call(
-        functools.partial(kernel, sizes),
-        out_shape=(
-            jax.ShapeDtypeStruct(adjoint_in.shape, f32),
-            jax.ShapeDtypeStruct(design.shape, f32),
-            jax.ShapeDtypeStruct((ey, ez), f32),
-        ),
-        in_specs=[any_spec] * 5,
-        out_specs=(vmem_spec, vmem_spec, vmem_spec),
-        scratch_shapes=[
+    else:
+        run = general_kernel
+        sum_scratch = []
+        for n in sum_groups(sizes):
+            sum_scratch += [
+                pltpu.VMEM((1, ez), f32),
+                pltpu.VMEM((n, ez), f32),
+                pltpu.SemaphoreType.DMA((max(n - 1, 1),)),
+                pltpu.SemaphoreType.DMA((max(n - 1, 1),)),
+            ]
+        scratch = [
             pltpu.VMEM(adjoint_in.shape, f32),
             pltpu.VMEM(forward_states.shape, f32),
             pltpu.VMEM(design.shape, f32),
@@ -634,7 +984,17 @@
             pltpu.SemaphoreType.DMA((2, 18)),
             pltpu.SemaphoreType.DMA((2, 18)),
             *sum_scratch,
-        ],
+        ]
+    adjoint, sens, tot = pl.pallas_call(
+        functools.partial(run, sizes),
+        out_shape=(
+            jax.ShapeDtypeStruct(adjoint_in.shape, f32),
+            jax.ShapeDtypeStruct(design.shape, f32),
+            jax.ShapeDtypeStruct((ey, ez), f32),
+        ),
+        in_specs=[any_spec] * 5,
+        out_specs=(vmem_spec, vmem_spec, vmem_spec),
+        scratch_shapes=scratch,
         compiler_params=pltpu.CompilerParams(
             collective_id=0, has_side_effects=True, vmem_limit_bytes=VMEM_LIMIT
         ),

time: 20.9 us -> 19.1 us (0.914)
  Pallas kernels: 20.1 us -> 18.3 us
    pallas_call x1, Pallas kernels: 19.2 us -> 17.5 us  [body(): pl.pallas_call(functools.partial(run, sizes), out_shape=(jax.ShapeDtypeSt...]
where the time goes in v1:
time: 19.1 us; the launch traced here: 19 us
  Pallas kernels  18.3 us (96%)
  between operations  0.64 us (3%)
    pallas_call x1, Pallas kernels, body(): pl.pallas_call(functools.partial(run, sizes), out_shape=(jax.ShapeDtypeSt...  17.5 us
    pallas_call x1, Pallas kernels, body(): pl.pallas_call(hand_on, out_shape=(jax.ShapeDtypeStruct(adjoint_in.shape,...  0.88 us

profile of v1, /device:TPU:0, one launch (start us, length us, event | category | flops | bytes accessed | tf_op | source)
XLA Modules:
  0.0 19.0 jit_solution(11582744293888777927)
XLA Ops:
  0.6 17.5 %shard_map.84 = (f32[19,8,8,128]{3,2,1,0:T(8,128)S(1)}, f32[8,8,128]{2,1,0:T(8,128)S(1)}, f32[8,128]{1,0:T(8,128)S(1)}) custom-call(f32[19,8,8,128]{3,2,1,0:T(8,128)} %adj_hbm.1, f32[2,19,8,8,128]{4,3,2,1,0:T(8,128)} %fwd_hbm.1, f32[8,8,128]{2,1,0:T(8,128)} %des_hbm.1, s32[8,8,128]{2,1,0:T(8,128)} %sol_hbm.1, s32[8,8,128]{2,1,0:T(8,128)} %kind_hbm.1), custom_call_target="tpu_custom_call" | custom-call | tf_op jit(solution)/shard_map/pallas_call | solution.py:988
  18.1 0.9 %shard_map.85 = (f32[19,8,8,128]{3,2,1,0:T(8,128)}, f32[8,8,128]{2,1,0:T(8,128)}, f32[1]{0:T(128)}, f32[1]{0:T(128)}) custom-call(f32[19,8,8,128]{3,2,1,0:T(8,128)S(1)} %get-tuple-element.11.adj_in, f32[8,8,128]{2,1,0:T(8,128)S(1)} %get-tuple-element.12.sens_in, f32[8,128]{1,0:T(8,128)S(1)} %get-tuple-element.13.tot_in), custom_call_target="tpu_custom_call" | custom-call | tf_op jit(solution)/shard_map/pallas_call | solution.py:1002

commit v2 on v1

--- a/solution.py
+++ b/solution.py
@@ -561,11 +561,8 @@
             copy.wait_recv()
         total = jnp.sum(got[...], axis=0, keepdims=True)
         sent += copies
-    cells = nx * ex * ny * ey * nz * ez
-    square = jnp.sum(jnp.where(first, total, 0.0), axis=1, keepdims=True)
-    cost = jnp.sum(jnp.where(first, 0.0, total), axis=1, keepdims=True)
-    rms = jnp.sqrt(square / cells + 1e-06)
-    tot_ref[...] = jnp.where(lane == 0, jnp.broadcast_to(cost / cells, (ey, ez)), jnp.broadcast_to(rms, (ey, ez)))
+    tot_ref[0, 0:1, :] = jnp.where(first, total, 0.0)
+    tot_ref[0, 1:2, :] = jnp.where(first, 0.0, total)
     for t in (1, 0):
         for i in live:
             ok, copy = hop(i, t)
@@ -574,9 +571,132 @@
         copy.wait_send()
 
 
+def sum_rows():
+    trace = (WROWS[4] + WROWS[5] + WROWS[6]) / 3
+    along = WROWS[4] - trace
+    across = (WROWS[5] - WROWS[6]) / 2
+    assert np.allclose(WROWS[5], trace - along / 2 + across)
+    rows = [WROWS[0], WROWS[1], WROWS[2], WROWS[3]]
+    rows += [3 * trace, 3 * along, 3 * across, 3 * WROWS[7], 3 * WROWS[8], 3 * WROWS[9]]
+    out = np.stack(rows)[:, :16]
+    out[np.abs(out) < 1e-12] = 0.0
+    return out
+
+
+SUM_ROWS = sum_rows()
+
+
+def plus(a, b):
+    if a is None or b is None:
+        return b if a is None else a
+    return a + b
+
+
+def minus(a, b):
+    if b is None:
+        return a
+    return -b if a is None else a - b
+
+
+def times(c, a):
+    return None if a is None else c * a
+
+
+def some_moments(p):
+    s = {i: plus(p[i], p[i + 1]) for i in range(1, 19, 2)}
+    d = {i: minus(p[i], p[i + 1]) for i in range(1, 19, 2)}
+    sxy, sxz, syz = plus(s[7], s[9]), plus(s[11], s[13]), plus(s[15], s[17])
+    axis_yz = plus(s[3], s[5])
+    axis = plus(s[1], axis_yz)
+    exy = plus(sxy, sxz)
+    edge = plus(exy, syz)
+    m = [None] * 19
+    m[0] = plus(plus(p[0], axis), edge)
+    m[1] = minus(minus(times(8.0, edge), times(11.0, axis)), times(30.0, p[0]))
+    m[2] = plus(minus(edge, times(4.0, axis)), times(12.0, p[0]))
+    a = minus(times(2.0, s[1]), axis_yz)
+    b = minus(exy, times(2.0, syz))
+    m[9] = plus(a, b)
+    m[10] = minus(b, times(2.0, a))
+    a = minus(s[3], s[5])
+    b = minus(sxy, sxz)
+    m[11] = plus(a, b)
+    m[12] = minus(b, times(2.0, a))
+    m[13] = minus(s[7], s[9])
+    m[14] = minus(s[15], s[17])
+    m[15] = minus(s[11], s[13])
+    xa, xb = plus(d[7], d[9]), plus(d[11], d[13])
+    ya, yb = minus(d[7], d[9]), plus(d[15], d[17])
+    za, zb = minus(d[11], d[13]), minus(d[15], d[17])
+    for k, axis_d, u, v in ((3, d[1], xa, xb), (5, d[3], ya, yb), (7, d[5], za, zb)):
+        e = plus(u, v)
+        m[k] = plus(axis_d, e)
+        m[k + 1] = minus(e, times(4.0, axis_d))
+    m[16] = minus(xa, xb)
+    m[17] = minus(yb, ya)
+    m[18] = minus(za, zb)
+    return m
+
+
+def cell_state(f, g, fluid, inlet, outlet, weight):
+    s, d = flux_sums(f)
+    rho = f[0]
+    for i in s:
+        rho = rho + s[i]
+    fx = d[1] + (d[7] + d[9]) + (d[11] + d[13])
+    fy = d[3] + (d[7] - d[9]) + (d[15] + d[17])
+    fz = d[5] + (d[11] - d[13]) + (d[15] - d[17])
+    below = 1.0 / (0.5 + 0.6 * g)
+    damping = (0.1 + g) * below
+    slope = 0.44 * (below * below)
+    inv = 1.0 / rho
+    b = [fx * inv, fy * inv, fz * inv]
+    u = [c * damping for c in b]
+    uu = u[0] * u[0] + u[1] * u[1] + u[2] * u[2]
+    wr = weight * rho
+    v = [jnp.where(inlet, c, a) for a, c in zip(u, (inflow_speed, 0.0, 0.0))]
+    scale = jnp.where(inlet, 0.0, jnp.where(outlet, 3.0, 3.0 * rho))
+    half = (0.5 * weight) * uu
+    state = v + [wr * c for c in u] + b + [scale, damping * inv, half, fluid * slope]
+    return state, fluid * (rho * half)
+
+
+def cell_sums(m, state, inner, outlet):
+    vx, vy, vz, wx, wy, wz, bx, by, bz, scale, di, half, slope = state
+    n = [None] * 19
+    for k in range(16):
+        rate = float(np.float32(RATES[k]))
+        n[k] = m[k] * jnp.where(inner, rate, 1.0) if np.any(SUM_ROWS[:, k]) else None
+    s0, sx, sy, sz, trace, along, across, xy, yz, xz = [combine(r, n) for r in SUM_ROWS]
+    xx = trace + along
+    side_on = trace - 0.5 * along
+    yy, zz = side_on + across, side_on - across
+    ax = sx + (xx * vx + xy * vy + xz * vz) - s0 * vx
+    ay = sy + (xy * vx + yy * vy + yz * vz) - s0 * vy
+    az = sz + (xz * vx + yz * vy + zz * vz) - s0 * vz
+    along_v = (ax + sx) * vx + (ay + sy) * vy + (az + sz) * vz
+    rho_bar = jnp.where(outlet, 0.0, s0 + 1.5 * along_v) + half
+    ux_bar, uy_bar, uz_bar = scale * ax + wx, scale * ay + wy, scale * az + wz
+    d_bar = ux_bar * bx + uy_bar * by + uz_bar * bz
+    extra = [rho_bar - d_bar * di, ux_bar * di, uy_bar * di, uz_bar * di]
+    return extra, d_bar * slope
+
+
+def cell_out(p, m, extra, inner, solid):
+    z = [None] * 19
+    for k in range(19):
+        coef = float(np.float32((1.0 - RATES[k]) / NORMS[k]))
+        z[k] = jnp.where(inner, coef * m[k], 0.0)
+    for k, e in zip((0, 3, 5, 7), extra):
+        z[k] = z[k] + e
+    out = rebuild(z)
+    return [jnp.where(solid, p[opposite_index[i]], out[i]) for i in range(19)]
+
+
 def near(sizes, cells):
     nx, ny, nz = sizes
-    return ny == 2 and nz == 2 and nx * ny * nz <= 64 and cells[0] == cells[1]
+    ex, ey, _ = cells
+    return ny == 2 and nz == 2 and nx * ny * nz <= 64 and ex == ey and ey % 8 == 0
 
 
 def rounds(nx):
@@ -598,7 +718,10 @@
     des,
     marks,
     mid,
+    pre,
+    mom,
     xs,
+    xe,
     ys,
     zs,
     xr,
@@ -625,8 +748,8 @@
         pltpu.make_async_copy(adj_hbm, adj, load_sem.at[0]),
         pltpu.make_async_copy(fwd_hbm, fwd, load_sem.at[1]),
         pltpu.make_async_copy(des_hbm, des, load_sem.at[2]),
-        pltpu.make_async_copy(sol_hbm, marks.at[0], load_sem.at[3]),
-        pltpu.make_async_copy(kind_hbm, marks.at[1], load_sem.at[3]),
+        pltpu.make_async_copy(sol_hbm, marks.at[0], load_sem.at[2]),
+        pltpu.make_async_copy(kind_hbm, marks.at[1], load_sem.at[2]),
     ]
     loads[0].start()
 
@@ -710,31 +833,36 @@
             device_id_type=MESH,
         )
 
-    def x_sends(t, s):
-        h = side(s)
-        sent, came = send_sem.at[h], face_sem.at[h, t]
-        slot = 1 + oy if s == 1 else 2 - oy
+    def x_sends(t, turn):
+        h = lax.rem(mx + turn, 2)
+        sent, came, at = send_sem.at[h], face_sem.at[h, t], mx - 1 + 2 * h
+        face, last = 5 * ey, 6 * ey
+        copies = [
+            push(zs.at[t], xr.at[h, t, pl.ds(face, ey)], sent, came, at, my, oz),
+            push(xs.at[t, h], xr.at[h, t, pl.ds(0, face)], sent, came, at, my, mz),
+            push(xe.at[t, h, oy], xr.at[h, t, pl.ds(last, 1)], sent, came, at, oy, mz),
+        ]
+        return jnp.where(h == 0, mx > 0, mx < nx - 1), copies
+
+    def side_sends(t):
+        sent, came = send_sem.at[2], side_sem.at[t]
         return [
-            push(zs.at[t], xr.at[h, t, 6], sent, came, mx - s, my, oz),
-            push(xs.at[t, h], xr.at[h, t, pl.ds(0, 5)], sent, came, mx - s, my, mz),
-            push(ys.at[t, oy, slot], xr.at[h, t, 5], sent, came, mx - s, oy, mz),
-        ]
-
-    def side_sends(t):
-        sent = send_sem.at[2]
-        return [
-            push(zs.at[t], er.at[t, oy, oz], sent, side_sem.at[2, t], mx, oy, oz),
-            push(zs.at[t], zr.at[t, oz], sent, side_sem.at[1, t], mx, my, oz),
-            push(ys.at[t, oy], yr.at[t, oy], sent, side_sem.at[0, t], mx, oy, mz),
+            push(zs.at[t], zr.at[t, oz], sent, came, mx, my, oz),
+            push(zs.at[t], er.at[t, oy, oz], sent, came, mx, oy, oz),
+            push(ys.at[t, oy], yr.at[t, oy], sent, came, mx, oy, mz),
         ]
 
     def pack_layer(t, x, tiles, pack):
         for sign in (1, -1):
             h = side(sign)
+            edge = 0 if sign == 1 else ey - 1
             if x == (0 if sign == 1 else ex - 1):
                 for k, i in enumerate(group(0, sign)):
-                    xs[t, h, k] = tiles(i)
-            edge = 0 if sign == 1 else ey - 1
+                    xs[t, h, k * ey : (k + 1) * ey, :] = tiles(i)
+                    cy = LAT[i][1]
+                    if cy:
+                        cut = 0 if cy == 1 else ey - 1
+                        xe[t, h, side(cy)] = tiles(i)[cut : cut + 1, :]
             for k, i in enumerate(group(1, sign)):
                 ys[t, h, k, x : x + 1, :] = tiles(i)[edge : edge + 1, :]
         for k, (i, j) in enumerate(zip(group(2, 1), group(2, -1))):
@@ -747,25 +875,28 @@
 
     def send_all(t, pack):
         zs[t] = pack
-        for s in (1, -1):
-
-            @pl.when(has[-s])
+        for turn in (0, 1):
+            ok, copies = x_sends(t, turn)
+
+            @pl.when(ok)
             def _():
-                for copy in x_sends(t, s):
+                for copy in copies:
                     copy.start()
 
         for copy in side_sends(t):
             copy.start()
 
+    def await_bytes(ref, sem):
+        pltpu.make_async_copy(ref, ref, sem).wait()
+
     def receive_sides(t):
-        for copy in side_sends(t)[::-1]:
-            copy.wait_recv()
-
-    def receive_face(t, s):
-        h = side(s)
-        ref = xr.at[h, t]
-        copy = push(ref, ref, send_sem.at[h], face_sem.at[h, t], mx, my, mz)
-        pl.when(has[s])(copy.wait_recv)
+        await_bytes(xr.at[0, t], side_sem.at[t])
+
+    def receive_faces(t):
+        for s in (-1, 1):
+            h = side(s)
+            ref = xr.at[h, t, pl.ds(0, 6 * ey + 1)]
+            pl.when(has[s])(functools.partial(await_bytes, ref, face_sem.at[h, t]))
 
     def shifted_columns(t):
         moved = {}
@@ -782,14 +913,19 @@
         cx, cy, cz = LAT[i]
         at = x + cx
         inside = 0 <= at < ex
-        tile = source[i, at] if inside else xr[side(cx), t, SLOT[0][i]]
+        if inside:
+            tile = source[i, at]
+        else:
+            k = SLOT[0][i] * ey
+            tile = xr[side(cx), t, k : k + ey, :]
         src = 0 if cx == 1 else ex - 1
         if cy:
             h = side(cy)
             if inside:
                 fill = yr[t, h, SLOT[1][i], at : at + 1, :]
             else:
-                fill = jnp.where(match_y[h], xr[side(cx), t, 5, src : src + 1, :], 0.0)
+                fill = xr[side(cx), t, 6 * ey : 6 * ey + 1, :]
+                fill = jnp.where(match_y[h], fill, 0.0)
             last = ey - 1 if cy == 1 else 0
             tile = jnp.where(row == last, fill, pltpu.roll(tile, (-cy) % ey, 0))
         if cz:
@@ -800,7 +936,8 @@
             elif inside:
                 pack, col = zr[t, h], col + at
             else:
-                pack = jnp.where(match_z[h], xr[side(cx), t, 6], 0.0)
+                pack = xr[side(cx), t, 5 * ey : 6 * ey, :]
+                pack = jnp.where(match_z[h], pack, 0.0)
                 col = col + src
             last = ez - 1 if cz == 1 else 0
             if (last - col) % ez:
@@ -811,46 +948,59 @@
     whole_x = nx * ex
     zero = jnp.zeros((ey, ez), jnp.float32)
 
-    def step(t, source, target, pack):
-        cost_sum, square_sum = zero, zero
-        with jax.named_scope(f"sides {t}"):
-            receive_sides(t)
+    def marked(x):
+        kind = marks[1, x]
+        return kind == 0, kind == 1, kind == 2, marks[0, x] == 1
+
+    def prepare(t):
+        total = zero
+        for x in range(ex):
+            _, inlet, outlet, solid = marked(x)
+            fluid = jnp.where(solid, 0.0, 1.0)
+            place = (mx * ex + x).astype(jnp.float32)
+            weight = 1.0 + 2.0 * place / (whole_x - 1)
+            f = [fwd[t, i, x] for i in range(19)]
+            state, cost = cell_state(f, des[x], fluid, inlet, outlet, weight)
+            for q, value in enumerate(state):
+                pre[q, x] = value
+            total = total + cost
+        return total
+
+    def is_late(i, x):
+        return not 0 <= x + LAT[i][0] < ex
+
+    def sums_of(m, x):
+        inner, _, outlet, _ = marked(x)
+        return cell_sums(m, [pre[q, x] for q in range(13)], inner, outlet)
+
+    edges = sorted({0, ex - 1})
+    inner_planes = range(1, ex - 1)
+
+    def pull(t, source, done):
+        receive_sides(t)
         if t == 1:
             relay(1)
         moved = shifted_columns(t)
-        for x in sorted(range(ex), key=lambda x: x in (0, ex - 1)):
-            with jax.named_scope(f"faces {t}"):
-                if x == 0:
-                    receive_face(t, -1)
-                if x == ex - 1:
-                    receive_face(t, 1)
-            g = des[x]
-            solid = marks[0, x] == 1
-            fluid = jnp.where(solid, 0.0, 1.0)
-            kind = marks[1, x]
-            inlet, outlet = kind == 1, kind == 2
-            inner = jnp.logical_not(jnp.logical_or(inlet, outlet))
-            below = 1.0 / (0.5 + 0.6 * g)
-            damping = (0.1 + g) * below
-            slope = 0.44 * (below * below)
-            place = (mx * ex + x).astype(jnp.float32)
-            weight = 1.0 + 2.0 * place / (whole_x - 1)
-            f = [fwd[t, i, x] for i in range(19)]
+        for x in inner_planes:
             p = [pulled_tile(source, t, i, x, moved) for i in range(19)]
-            out, sens, cost = cell_adjoint(
-                f, p, damping, slope, fluid, solid, inner, inlet, outlet, weight
-            )
-            for i in range(19):
-                target[i, x] = out[i]
-            cost_sum = cost_sum + cost
-            if t == 1:
-                sens_ref[x] = sens
-                pack = pack_layer(0, x, lambda i: out[i], pack)
-            else:
-                sens = sens + sens_ref[x]
-                sens_ref[x] = sens
-                square_sum = square_sum + sens * sens
-        return cost_sum, square_sum, pack
+            done(x, p, some_moments(p))
+        early = {}
+        for x in edges:
+            p = [
+                None if is_late(i, x) else pulled_tile(source, t, i, x, moved)
+                for i in range(19)
+            ]
+            early[x] = p, some_moments(p)
+        with jax.named_scope(f"faces {t}"):
+            receive_faces(t)
+        for x in edges:
+            p, m = early[x]
+            late = [
+                pulled_tile(source, t, i, x, moved) if is_late(i, x) else None
+                for i in range(19)
+            ]
+            p = [b if a is None else a for a, b in zip(p, late)]
+            done(x, p, [plus(a, b) for a, b in zip(m, some_moments(late))])
 
     with jax.named_scope("load"):
         loads[0].wait()
@@ -862,17 +1012,43 @@
     with jax.named_scope("send 1"):
         send_all(1, pack)
         relay(0)
-    for load in loads[1:3]:
-        load.wait()
-    pltpu.make_async_copy(marks, marks, load_sem.at[3]).wait()
-    cost_one, _, pack = step(1, adj, mid, zero)
+    loads[1].wait()
+    await_bytes(fwd.at[0, pl.ds(0, 3)], load_sem.at[2])
+    cost = prepare(1)
+    packs = [zero]
+
+    def first_done(x, p, m):
+        inner, _, _, solid = marked(x)
+        extra, sens = sums_of(m, x)
+        out = cell_out(p, m, extra, inner, solid)
+        for i in range(19):
+            mid[i, x] = out[i]
+        sens_ref[x] = sens
+        packs[0] = pack_layer(0, x, lambda i: out[i], packs[0])
+
+    with jax.named_scope("step 1"):
+        pull(1, adj, first_done)
     with jax.named_scope("send 0"):
-        send_all(0, pack)
+        send_all(0, packs[0])
     for j in range(2, rounds(nx)):
         relay(j)
-    cost_two, square, _ = step(0, mid, out_ref, None)
-    part[0:1, :] = jnp.sum(square, axis=0, keepdims=True)
-    part[1:2, :] = jnp.sum(cost_one + cost_two, axis=0, keepdims=True)
+    cost = cost + prepare(0)
+    squares = [zero]
+
+    def second_done(x, p, m):
+        extra, sens = sums_of(m, x)
+        sens = sens + sens_ref[x]
+        sens_ref[x] = sens
+        squares[0] = squares[0] + sens * sens
+        for i in range(19):
+            adj[i, x] = p[i]
+        for k, value in enumerate(m + extra):
+            mom[k, x] = value
+
+    with jax.named_scope("step 0"):
+        pull(0, mid, second_done)
+    part[0:1, :] = jnp.sum(squares[0], axis=0, keepdims=True)
+    part[1:2, :] = jnp.sum(cost, axis=0, keepdims=True)
 
     with jax.named_scope("heard"):
         if rounds(nx):
@@ -888,34 +1064,52 @@
                 y, z = (oy if dy else my), (oz if dz else mz)
                 push(part, got.at[k - 1], sum_sem.at[0], sum_sem.at[1], px, y, z).start()
     got[n - 1] = part[...]
+    with jax.named_scope("out"):
+        for x in range(ex):
+            inner, _, _, solid = marked(x)
+            m = [mom[k, x] for k in range(23)]
+            out = cell_out([adj[i, x] for i in range(19)], m[:19], m[19:], inner, solid)
+            for i in range(19):
+                out_ref[i, x] = out[i]
     every = got.at[pl.ds(0, n - 1)]
     sums = push(every, every, sum_sem.at[0], sum_sem.at[1], mx, my, mz)
     with jax.named_scope("sums"):
         sums.wait_recv()
-    total = jnp.sum(jnp.sum(got[...], axis=0), axis=1, keepdims=True)
-    cells = nx * ex * ny * ey * nz * ez
-    rms = jnp.broadcast_to(jnp.sqrt(total[0:1] / cells + 1e-06), (ey, ez))
-    cost = jnp.broadcast_to(total[1:2] / cells, (ey, ez))
-    tot_ref[...] = jnp.where(lane == 0, cost, rms)
+    tot_ref[...] = got[...]
     with jax.named_scope("drain"):
         for s in (1, -1):
             h = side(s)
-            copy = push(xr.at[h], xr.at[h], send_sem.at[h], sum_sem.at[1], mx, my, mz)
-            pl.when(has[-s])(copy.wait_send)
-        push(xr.at[0], xr.at[0], send_sem.at[2], sum_sem.at[1], mx, my, mz).wait_send()
+            ref = xr.at[h, :, pl.ds(0, 6 * ey + 1)]
+            pl.when(has[-s])(functools.partial(await_bytes, ref, send_sem.at[h]))
+        await_bytes(xr.at[0], send_sem.at[2])
         sums.wait_send()
 
 
-def hand_on(adj_in, sens_in, tot_in, adj_out, sens_out, obj_out, rms_out, sens, obj, rms, sem):
+def hand_on(
+    cells,
+    adj_in,
+    sens_in,
+    sums_in,
+    adj_out,
+    sens_out,
+    obj_out,
+    rms_out,
+    sens,
+    obj,
+    rms,
+    sem,
+):
     moves = [(adj_in, adj_out), (sens, sens_out), (obj, obj_out), (rms, rms_out)]
     copies = [pltpu.make_async_copy(a, b, sem.at[k]) for k, (a, b) in enumerate(moves)]
     copies[0].start()
-    scale = jnp.broadcast_to(1.0 / tot_in[0:1, 1:2], tot_in.shape)
+    total = jnp.sum(jnp.sum(sums_in[...], axis=0), axis=1, keepdims=True) / cells
+    root = jnp.sqrt(total[0:1] + 1e-06)
+    scale = jnp.broadcast_to(1.0 / root, sens.shape[1:])
     for x in range(sens.shape[0]):
         sens[x] = sens_in[x] * scale
     copies[1].start()
-    obj[0] = tot_in[0, 0]
-    rms[0] = tot_in[0, 1]
+    obj[0] = total[1, 0]
+    rms[0] = root[0, 0]
     copies[2].start()
     copies[3].start()
     for copy in copies:
@@ -939,23 +1133,27 @@
             pltpu.VMEM(design.shape, f32),
             pltpu.VMEM((2, *design.shape), jnp.int32),
             pltpu.VMEM(adjoint_in.shape, f32),
-            pltpu.VMEM((2, 2, 5, ey, ez), f32),
+            pltpu.VMEM((13, *design.shape), f32),
+            pltpu.VMEM((23, *design.shape), f32),
+            pltpu.VMEM((2, 2, 5 * ey, ez), f32),
+            pltpu.VMEM((2, 2, 2, 1, ez), f32),
             pltpu.VMEM((2, 2, 5, ex, ez), f32),
             pltpu.VMEM((2, ey, ez), f32),
-            pltpu.VMEM((2, 2, 7, ey, ez), f32),
+            pltpu.VMEM((2, 2, 7 * ey, ez), f32),
             pltpu.VMEM((2, 2, 5, ex, ez), f32),
             pltpu.VMEM((2, 2, ey, ez), f32),
             pltpu.VMEM((2, 2, 2, ey, ez), f32),
             pltpu.VMEM((2, ez), f32),
             pltpu.VMEM((n, 2, ez), f32),
-            pltpu.SemaphoreType.DMA((4,)),
             pltpu.SemaphoreType.DMA((3,)),
-            pltpu.SemaphoreType.DMA((3, 2)),
+            pltpu.SemaphoreType.DMA((3,)),
+            pltpu.SemaphoreType.DMA((2,)),
             pltpu.SemaphoreType.DMA((2, 2)),
             pltpu.SemaphoreType.DMA((2,)),
             pltpu.SemaphoreType.REGULAR((max(rounds(nx), 1),)),
         ]
     else:
+        n = 1
         run = general_kernel
         sum_scratch = []
         for n in sum_groups(sizes):
@@ -990,7 +1188,7 @@
         out_shape=(
             jax.ShapeDtypeStruct(adjoint_in.shape, f32),
             jax.ShapeDtypeStruct(design.shape, f32),
-            jax.ShapeDtypeStruct((ey, ez), f32),
+            jax.ShapeDtypeStruct((n, 2, ez), f32),
         ),
         in_specs=[any_spec] * 5,
         out_specs=(vmem_spec, vmem_spec, vmem_spec),
@@ -1000,7 +1198,7 @@
         ),
     )(*operands)
     adjoint, sens, objective, rms = pl.pallas_call(
-        hand_on,
+        functools.partial(hand_on, nx * ex * ny * ey * nz * ez),
         out_shape=(
             jax.ShapeDtypeStruct(adjoint_in.shape, f32),
             jax.ShapeDtypeStruct(design.shape, f32),

time: 19.1 us -> 18.7 us (0.979)
  Pallas kernels: 18.3 us -> 17.9 us
    pallas_call x1, Pallas kernels: 17.5 us -> 17 us  [body(): pl.pallas_call(functools.partial(run, sizes), out_shape=(jax.ShapeDtypeSt...]
where the time goes in v2:
time: 18.7 us; the launch traced here: 18.6 us
  Pallas kernels  17.9 us (96%)
  between operations  0.64 us (3%)
    pallas_call x1, Pallas kernels, body(): pl.pallas_call(functools.partial(run, sizes), out_shape=(jax.ShapeDtypeSt...  17 us
    pallas_call x1, Pallas kernels, body(): pl.pallas_call(functools.partial(hand_on, nx * ex * ny * ey * nz * ez), o...  0.89 us

profile of v2, /device:TPU:0, one launch (start us, length us, event | category | flops | bytes accessed | tf_op | source)
XLA Modules:
  0.0 18.6 jit_solution(10358754836993433445)
XLA Ops:
  0.6 17.0 %shard_map.84 = (f32[19,8,8,128]{3,2,1,0:T(8,128)S(1)}, f32[8,8,128]{2,1,0:T(8,128)S(1)}, f32[32,2,128]{2,1,0:T(2,128)S(1)}) custom-call(f32[19,8,8,128]{3,2,1,0:T(8,128)} %adj_hbm.1, f32[2,19,8,8,128]{4,3,2,1,0:T(8,128)} %fwd_hbm.1, f32[8,8,128]{2,1,0:T(8,128)} %des_hbm.1, s32[8,8,128]{2,1,0:T(8,128)} %sol_hbm.1, s32[8,8,128]{2,1,0:T(8,128)} %kind_hbm.1), custom_call_target="tpu_custom_call" | custom-call | tf_op jit(solution)/shard_map/pallas_call | solution.py:1186
  17.7 0.9 %shard_map.85 = (f32[19,8,8,128]{3,2,1,0:T(8,128)}, f32[8,8,128]{2,1,0:T(8,128)}, f32[1]{0:T(128)}, f32[1]{0:T(128)}) custom-call(f32[19,8,8,128]{3,2,1,0:T(8,128)S(1)} %get-tuple-element.11.adj_in, f32[8,8,128]{2,1,0:T(8,128)S(1)} %get-tuple-element.12.sens_in, f32[32,2,128]{2,1,0:T(2,128)S(1)} %get-tuple-element.13.sums_in), custom_call_target="tpu_custom_call" | custom-call | tf_op jit(solution)/shard_map/pallas_call | solution.py:1200

commit v3 on v2

--- a/solution.py
+++ b/solution.py
@@ -703,6 +703,10 @@
     return max((nx - 1) // 2, 0)
 
 
+def end_rows(n, ey, faces):
+    return 2 * (7 * ey + faces * (6 * ey + 1)) + 2 * (n - 1)
+
+
 def fast_kernel(
     sizes,
     adj_hbm,
@@ -729,7 +733,8 @@
     zr,
     er,
     part,
-    got,
+    size_loads,
+    size_sends,
     load_sem,
     send_sem,
     side_sem,
@@ -747,9 +752,9 @@
     loads = [
         pltpu.make_async_copy(adj_hbm, adj, load_sem.at[0]),
         pltpu.make_async_copy(fwd_hbm, fwd, load_sem.at[1]),
-        pltpu.make_async_copy(des_hbm, des, load_sem.at[2]),
-        pltpu.make_async_copy(sol_hbm, marks.at[0], load_sem.at[2]),
-        pltpu.make_async_copy(kind_hbm, marks.at[1], load_sem.at[2]),
+        pltpu.make_async_copy(des_hbm, des, load_sem.at[1]),
+        pltpu.make_async_copy(sol_hbm, marks.at[0], load_sem.at[1]),
+        pltpu.make_async_copy(kind_hbm, marks.at[1], load_sem.at[1]),
     ]
     loads[0].start()
 
@@ -760,13 +765,9 @@
             barrier, inc=1, device_id={"gx": x, "gy": y, "gz": z}, device_id_type=MESH
         )
 
-    for s in (1, -1):
-
-        @pl.when(has[s])
-        def _():
-            for y, z in ((my, oz), (oy, oz), (oy, mz), (my, mz)):
-                greet(mx + s, y, z)
-
+    for y, z in ((my, oz), (oy, oz), (my, mz), (oy, mz)):
+        for s in (1, -1):
+            pl.when(has[s])(functools.partial(greet, mx + s, y, z))
     for y, z in ((my, oz), (oy, oz), (oy, mz)):
         greet(mx, y, z)
     for s in (2, -2):
@@ -835,34 +836,44 @@
 
     def x_sends(t, turn):
         h = lax.rem(mx + turn, 2)
-        sent, came, at = send_sem.at[h], face_sem.at[h, t], mx - 1 + 2 * h
+        sent, came, at = send_sem, face_sem.at[t], mx - 1 + 2 * h
         face, last = 5 * ey, 6 * ey
+        tilted = pl.multiple_of((3 + jnp.where(h == 0, oz, mz)) * ey, 8)
+        edge = xs.at[t, h, pl.ds(tilted, ey)]
         copies = [
-            push(zs.at[t], xr.at[h, t, pl.ds(face, ey)], sent, came, at, my, oz),
+            push(edge, xr.at[h, t, pl.ds(face, ey)], sent, came, at, my, oz),
             push(xs.at[t, h], xr.at[h, t, pl.ds(0, face)], sent, came, at, my, mz),
             push(xe.at[t, h, oy], xr.at[h, t, pl.ds(last, 1)], sent, came, at, oy, mz),
         ]
         return jnp.where(h == 0, mx > 0, mx < nx - 1), copies
 
     def side_sends(t):
-        sent, came = send_sem.at[2], side_sem.at[t]
+        sent, came = send_sem, side_sem.at[t]
         return [
             push(zs.at[t], zr.at[t, oz], sent, came, mx, my, oz),
             push(zs.at[t], er.at[t, oy, oz], sent, came, mx, oy, oz),
             push(ys.at[t, oy], yr.at[t, oy], sent, came, mx, oy, mz),
         ]
 
-    def pack_layer(t, x, tiles, pack):
+    shifted = (1,)
+
+    def store_face(t, x, tiles):
+        for sign in (1, -1):
+            h = side(sign)
+            if x != (0 if sign == 1 else ex - 1):
+                continue
+            for k, i in enumerate(group(0, sign)):
+                cy, cz = LAT[i][1:]
+                sent = pltpu.roll(tiles(i), (-cz) % ez, 1) if cz and t in shifted else tiles(i)
+                xs[t, h, k * ey : (k + 1) * ey, :] = sent
+                if cy:
+                    cut = 0 if cy == 1 else ey - 1
+                    xe[t, h, side(cy)] = tiles(i)[cut : cut + 1, :]
+
+    def pack_sides(t, x, tiles, pack):
         for sign in (1, -1):
             h = side(sign)
             edge = 0 if sign == 1 else ey - 1
-            if x == (0 if sign == 1 else ex - 1):
-                for k, i in enumerate(group(0, sign)):
-                    xs[t, h, k * ey : (k + 1) * ey, :] = tiles(i)
-                    cy = LAT[i][1]
-                    if cy:
-                        cut = 0 if cy == 1 else ey - 1
-                        xe[t, h, side(cy)] = tiles(i)[cut : cut + 1, :]
             for k, i in enumerate(group(1, sign)):
                 ys[t, h, k, x : x + 1, :] = tiles(i)[edge : edge + 1, :]
         for k, (i, j) in enumerate(zip(group(2, 1), group(2, -1))):
@@ -873,8 +884,7 @@
             pack = jnp.where(slot_lane == at, moved, pack)
         return pack
 
-    def send_all(t, pack):
-        zs[t] = pack
+    def send_faces(t):
         for turn in (0, 1):
             ok, copies = x_sends(t, turn)
 
@@ -883,6 +893,8 @@
                 for copy in copies:
                     copy.start()
 
+    def send_sides(t, pack):
+        zs[t] = pack
         for copy in side_sends(t):
             copy.start()
 
@@ -892,11 +904,20 @@
     def receive_sides(t):
         await_bytes(xr.at[0, t], side_sem.at[t])
 
+    both = jnp.logical_and(has[1], has[-1])
+
     def receive_faces(t):
-        for s in (-1, 1):
-            h = side(s)
-            ref = xr.at[h, t, pl.ds(0, 6 * ey + 1)]
-            pl.when(has[s])(functools.partial(await_bytes, ref, face_sem.at[h, t]))
+        rows = pl.ds(0, 6 * ey + 1)
+
+        @pl.when(both)
+        def _():
+            await_bytes(xr.at[:, t, rows], face_sem.at[t])
+
+        if nx > 1:
+
+            @pl.when(jnp.logical_not(both))
+            def _():
+                await_bytes(xr.at[0, t, rows], face_sem.at[t])
 
     def shifted_columns(t):
         moved = {}
@@ -930,16 +951,19 @@
             tile = jnp.where(row == last, fill, pltpu.roll(tile, (-cy) % ey, 0))
         if cz:
             h = side(cz)
+            last = ez - 1 if cz == 1 else 0
+            if not inside:
+                pack = xr[side(cx), t, 5 * ey : 6 * ey, :]
+                pack = jnp.where(match_z[h], pack, 0.0)
+                if t in shifted:
+                    return jnp.where(lane == last, pack, tile)
+                tile = jnp.where(lane == ez - 1 - last, pack, tile)
+                return pltpu.roll(tile, (-cz) % ez, 1)
             col = SLOT[2][i] * ex - h
             if cy:
                 pack, col = moved[i], col + x
-            elif inside:
+            else:
                 pack, col = zr[t, h], col + at
-            else:
-                pack = xr[side(cx), t, 5 * ey : 6 * ey, :]
-                pack = jnp.where(match_z[h], pack, 0.0)
-                col = col + src
-            last = ez - 1 if cz == 1 else 0
             if (last - col) % ez:
                 pack = pltpu.roll(pack, (last - col) % ez, 1)
             tile = jnp.where(lane == last, pack, pltpu.roll(tile, (-cz) % ez, 1))
@@ -1004,32 +1028,47 @@
 
     with jax.named_scope("load"):
         loads[0].wait()
-    pack = zero
-    for x in range(ex):
-        pack = pack_layer(1, x, lambda i: adj[i, x], pack)
+    for x in edges:
+        store_face(1, x, lambda i: adj[i, x])
     with jax.named_scope("greeted"):
         pl.semaphore_wait(barrier, count)
     with jax.named_scope("send 1"):
-        send_all(1, pack)
+        send_faces(1)
+    pack = zero
+    for x in range(ex):
+        pack = pack_sides(1, x, lambda i: adj[i, x], pack)
+    with jax.named_scope("sides 1"):
+        send_sides(1, pack)
         relay(0)
-    loads[1].wait()
-    await_bytes(fwd.at[0, pl.ds(0, 3)], load_sem.at[2])
+    await_bytes(size_loads, load_sem.at[1])
     cost = prepare(1)
     packs = [zero]
+    kept = {}
+
+    def keep(x, out, sens):
+        for i in range(19):
+            mid[i, x] = out[i]
+        sens_ref[x] = sens
+        packs[0] = pack_sides(0, x, lambda i: out[i], packs[0])
 
     def first_done(x, p, m):
         inner, _, _, solid = marked(x)
         extra, sens = sums_of(m, x)
         out = cell_out(p, m, extra, inner, solid)
-        for i in range(19):
-            mid[i, x] = out[i]
-        sens_ref[x] = sens
-        packs[0] = pack_layer(0, x, lambda i: out[i], packs[0])
+        if x in edges:
+            store_face(0, x, lambda i: out[i])
+            kept[x] = out, sens
+        else:
+            keep(x, out, sens)
 
     with jax.named_scope("step 1"):
         pull(1, adj, first_done)
     with jax.named_scope("send 0"):
-        send_all(0, packs[0])
+        send_faces(0)
+    for x, (out, sens) in kept.items():
+        keep(x, out, sens)
+    with jax.named_scope("sides 0"):
+        send_sides(0, packs[0])
     for j in range(2, rounds(nx)):
         relay(j)
     cost = cost + prepare(0)
@@ -1054,16 +1093,21 @@
         if rounds(nx):
             hear(rounds(nx) - 1)
     n = nx * ny * nz
+
+    def sum_send(k, x, y, z):
+        return push(part, tot_ref.at[k - 1], send_sem, sum_sem, x, y, z)
+
     with jax.named_scope("send sums"):
-        for dx in sorted(range(nx), key=lambda d: (d == 0, min(d, nx - d))):
-            px = jnp.where(mx + dx >= nx, mx + dx - nx, mx + dx)
-            for dy, dz in ((1, 1), (0, 1), (1, 0), (0, 0)):
+        for px in range(nx):
+            dx = jnp.where(px < mx, px - mx + nx, px - mx)
+            for dy, dz in ((0, 1), (1, 1), (0, 0), (1, 0)):
                 k = (dx * ny + dy) * nz + dz
-                if k == 0:
-                    continue
                 y, z = (oy if dy else my), (oz if dz else mz)
-                push(part, got.at[k - 1], sum_sem.at[0], sum_sem.at[1], px, y, z).start()
-    got[n - 1] = part[...]
+                if dy or dz:
+                    sum_send(k, px, y, z).start()
+                else:
+                    pl.when(px != mx)(sum_send(k, px, y, z).start)
+    tot_ref[n - 1] = part[...]
     with jax.named_scope("out"):
         for x in range(ex):
             inner, _, _, solid = marked(x)
@@ -1071,18 +1115,17 @@
             out = cell_out([adj[i, x] for i in range(19)], m[:19], m[19:], inner, solid)
             for i in range(19):
                 out_ref[i, x] = out[i]
-    every = got.at[pl.ds(0, n - 1)]
-    sums = push(every, every, sum_sem.at[0], sum_sem.at[1], mx, my, mz)
     with jax.named_scope("sums"):
-        sums.wait_recv()
-    tot_ref[...] = got[...]
+        await_bytes(tot_ref.at[pl.ds(0, n - 1)], sum_sem)
     with jax.named_scope("drain"):
-        for s in (1, -1):
-            h = side(s)
-            ref = xr.at[h, :, pl.ds(0, 6 * ey + 1)]
-            pl.when(has[-s])(functools.partial(await_bytes, ref, send_sem.at[h]))
-        await_bytes(xr.at[0], send_sem.at[2])
-        sums.wait_send()
+
+        @pl.when(both)
+        def _():
+            await_bytes(size_sends, send_sem)
+
+        @pl.when(jnp.logical_not(both))
+        def _():
+            await_bytes(size_sends.at[pl.ds(0, end_rows(n, ey, nx > 1))], send_sem)
 
 
 def hand_on(
@@ -1126,6 +1169,7 @@
     operands = [pltpu.with_memory_space_constraint(a, pltpu.HBM) for a in operands]
     if near(sizes, design.shape):
         n = nx * ny * nz
+        count = adjoint_in.shape[0]
         run = fast_kernel
         scratch = [
             pltpu.VMEM(adjoint_in.shape, f32),
@@ -1144,12 +1188,13 @@
             pltpu.VMEM((2, 2, ey, ez), f32),
             pltpu.VMEM((2, 2, 2, ey, ez), f32),
             pltpu.VMEM((2, ez), f32),
-            pltpu.VMEM((n, 2, ez), f32),
-            pltpu.SemaphoreType.DMA((3,)),
-            pltpu.SemaphoreType.DMA((3,)),
+            pltpu.VMEM((2 * count + 3, *design.shape), f32),
+            pltpu.VMEM((end_rows(n, ey, 2), ez), f32),
             pltpu.SemaphoreType.DMA((2,)),
-            pltpu.SemaphoreType.DMA((2, 2)),
+            pltpu.SemaphoreType.DMA,
             pltpu.SemaphoreType.DMA((2,)),
+            pltpu.SemaphoreType.DMA((2,)),
+            pltpu.SemaphoreType.DMA,
             pltpu.SemaphoreType.REGULAR((max(rounds(nx), 1),)),
         ]
     else:

time: 18.7 us -> 18.4 us (0.984)
  Pallas kernels: 17.9 us -> 17.6 us
    pallas_call x1, Pallas kernels: 17 us -> 16.7 us  [body(): pl.pallas_call(functools.partial(run, sizes), out_shape=(jax.ShapeDtypeSt...]
where the time goes in v3:
time: 18.4 us; the launch traced here: 18.2 us
  Pallas kernels  17.6 us (96%)
  between operations  0.64 us (3%)
    pallas_call x1, Pallas kernels, body(): pl.pallas_call(functools.partial(run, sizes), out_shape=(jax.ShapeDtypeSt...  16.7 us
    pallas_call x1, Pallas kernels, body(): pl.pallas_call(functools.partial(hand_on, nx * ex * ny * ey * nz * ez), o...  0.89 us

profile of v3, /device:TPU:0, one launch (start us, length us, event | category | flops | bytes accessed | tf_op | source)
XLA Modules:
  0.0 18.2 jit_solution(2670362743542715740)
XLA Ops:
  0.6 16.7 %shard_map.84 = (f32[19,8,8,128]{3,2,1,0:T(8,128)S(1)}, f32[8,8,128]{2,1,0:T(8,128)S(1)}, f32[32,2,128]{2,1,0:T(2,128)S(1)}) custom-call(f32[19,8,8,128]{3,2,1,0:T(8,128)} %adj_hbm.1, f32[2,19,8,8,128]{4,3,2,1,0:T(8,128)} %fwd_hbm.1, f32[8,8,128]{2,1,0:T(8,128)} %des_hbm.1, s32[8,8,128]{2,1,0:T(8,128)} %sol_hbm.1, s32[8,8,128]{2,1,0:T(8,128)} %kind_hbm.1), custom_call_target="tpu_custom_call" | custom-call | tf_op jit(solution)/shard_map/pallas_call | solution.py:1231
  17.3 0.9 %shard_map.85 = (f32[19,8,8,128]{3,2,1,0:T(8,128)}, f32[8,8,128]{2,1,0:T(8,128)}, f32[1]{0:T(128)}, f32[1]{0:T(128)}) custom-call(f32[19,8,8,128]{3,2,1,0:T(8,128)S(1)} %get-tuple-element.11.adj_in, f32[8,8,128]{2,1,0:T(8,128)S(1)} %get-tuple-element.12.sens_in, f32[32,2,128]{2,1,0:T(2,128)S(1)} %get-tuple-element.13.sums_in), custom_call_target="tpu_custom_call" | custom-call | tf_op jit(solution)/shard_map/pallas_call | solution.py:1245

commit v4 on v3

--- a/solution.py
+++ b/solution.py
@@ -1169,6 +1169,7 @@
     operands = [pltpu.with_memory_space_constraint(a, pltpu.HBM) for a in operands]
     if near(sizes, design.shape):
         n = nx * ny * nz
+        entries = n
         count = adjoint_in.shape[0]
         run = fast_kernel
         scratch = [
@@ -1198,7 +1199,7 @@
             pltpu.SemaphoreType.REGULAR((max(rounds(nx), 1),)),
         ]
     else:
-        n = 1
+        entries = 1
         run = general_kernel
         sum_scratch = []
         for n in sum_groups(sizes):
@@ -1233,7 +1234,7 @@
         out_shape=(
             jax.ShapeDtypeStruct(adjoint_in.shape, f32),
             jax.ShapeDtypeStruct(design.shape, f32),
-            jax.ShapeDtypeStruct((n, 2, ez), f32),
+            jax.ShapeDtypeStruct((entries, 2, ez), f32),
         ),
         in_specs=[any_spec] * 5,
         out_specs=(vmem_spec, vmem_spec, vmem_spec),

time: 18.4 us -> 18.4 us (level)
  no operation moved by 1% of the time
where the time goes in v4:
time: 18.4 us; the launch traced here: 18.2 us
  Pallas kernels  17.6 us (96%)
  between operations  0.64 us (3%)
    pallas_call x1, Pallas kernels, body(): pl.pallas_call(functools.partial(run, sizes), out_shape=(jax.ShapeDtypeSt...  16.7 us
    pallas_call x1, Pallas kernels, body(): pl.pallas_call(functools.partial(hand_on, nx * ex * ny * ey * nz * ez), o...  0.89 us

profile of v4, /device:TPU:0, one launch (start us, length us, event | category | flops | bytes accessed | tf_op | source)
XLA Modules:
  0.0 18.2 jit_solution(2670362743542715740)
XLA Ops:
  0.6 16.7 %shard_map.84 = (f32[19,8,8,128]{3,2,1,0:T(8,128)S(1)}, f32[8,8,128]{2,1,0:T(8,128)S(1)}, f32[32,2,128]{2,1,0:T(2,128)S(1)}) custom-call(f32[19,8,8,128]{3,2,1,0:T(8,128)} %adj_hbm.1, f32[2,19,8,8,128]{4,3,2,1,0:T(8,128)} %fwd_hbm.1, f32[8,8,128]{2,1,0:T(8,128)} %des_hbm.1, s32[8,8,128]{2,1,0:T(8,128)} %sol_hbm.1, s32[8,8,128]{2,1,0:T(8,128)} %kind_hbm.1), custom_call_target="tpu_custom_call" | custom-call | tf_op jit(solution)/shard_map/pallas_call | solution.py:1232
  17.3 0.9 %shard_map.85 = (f32[19,8,8,128]{3,2,1,0:T(8,128)}, f32[8,8,128]{2,1,0:T(8,128)}, f32[1]{0:T(128)}, f32[1]{0:T(128)}) custom-call(f32[19,8,8,128]{3,2,1,0:T(8,128)S(1)} %get-tuple-element.11.adj_in, f32[8,8,128]{2,1,0:T(8,128)S(1)} %get-tuple-element.12.sens_in, f32[32,2,128]{2,1,0:T(2,128)S(1)} %get-tuple-element.13.sums_in), custom_call_target="tpu_custom_call" | custom-call | tf_op jit(solution)/shard_map/pallas_call | solution.py:1246

commit v5 on v4

--- a/solution.py
+++ b/solution.py
@@ -885,13 +885,9 @@
         return pack
 
     def send_faces(t):
-        for turn in (0, 1):
+        for k, turn in ((0, 0), (0, 1), (2, 0), (2, 1), (1, 0), (1, 1)):
             ok, copies = x_sends(t, turn)
-
-            @pl.when(ok)
-            def _():
-                for copy in copies:
-                    copy.start()
+            pl.when(ok)(copies[k].start)
 
     def send_sides(t, pack):
         zs[t] = pack

time: 18.4 us -> 18.4 us (level)
  no operation moved by 1% of the time
where the time goes in v5:
time: 18.4 us; the launch traced here: 18.2 us
  Pallas kernels  17.6 us (96%)
  between operations  0.64 us (3%)
    pallas_call x1, Pallas kernels, body(): pl.pallas_call(functools.partial(run, sizes), out_shape=(jax.ShapeDtypeSt...  16.7 us
    pallas_call x1, Pallas kernels, body(): pl.pallas_call(functools.partial(hand_on, nx * ex * ny * ey * nz * ez), o...  0.89 us

profile of v5, /device:TPU:0, one launch (start us, length us, event | category | flops | bytes accessed | tf_op | source)
XLA Modules:
  0.0 18.2 jit_solution(3908790050158489834)
XLA Ops:
  0.6 16.7 %shard_map.84 = (f32[19,8,8,128]{3,2,1,0:T(8,128)S(1)}, f32[8,8,128]{2,1,0:T(8,128)S(1)}, f32[32,2,128]{2,1,0:T(2,128)S(1)}) custom-call(f32[19,8,8,128]{3,2,1,0:T(8,128)} %adj_hbm.1, f32[2,19,8,8,128]{4,3,2,1,0:T(8,128)} %fwd_hbm.1, f32[8,8,128]{2,1,0:T(8,128)} %des_hbm.1, s32[8,8,128]{2,1,0:T(8,128)} %sol_hbm.1, s32[8,8,128]{2,1,0:T(8,128)} %kind_hbm.1), custom_call_target="tpu_custom_call" | custom-call | tf_op jit(solution)/shard_map/pallas_call | solution.py:1228
  17.3 0.9 %shard_map.85 = (f32[19,8,8,128]{3,2,1,0:T(8,128)}, f32[8,8,128]{2,1,0:T(8,128)}, f32[1]{0:T(128)}, f32[1]{0:T(128)}) custom-call(f32[19,8,8,128]{3,2,1,0:T(8,128)S(1)} %get-tuple-element.11.adj_in, f32[8,8,128]{2,1,0:T(8,128)S(1)} %get-tuple-element.12.sens_in, f32[32,2,128]{2,1,0:T(2,128)S(1)} %get-tuple-element.13.sums_in), custom_call_target="tpu_custom_call" | custom-call | tf_op jit(solution)/shard_map/pallas_call | solution.py:1242
